TPU v7x, 32 devices: a whole 2x2x4 slice. The times are simulated.
32 devices in a mesh: node: 8 (over z, x), expert: 4 (over y, core).
Axes of the slice: x: 2, y: 2, z: 4, core: 2. Of those that a mesh axis runs over, the one named last changes fastest.
Arguments:
- param_gu: float32 [32768, 1024], P('node', 'expert'), may hold values from -13 to 13
- param_down: float32 [1024, 16384], P('node', 'expert'), may hold values from -13 to 13
- tokens: bfloat16 [4096, 4096], P(('node', 'expert')), may hold values from -6 to 6
- cotangent: bfloat16 [4096, 4096], P(('node', 'expert')), may hold values from -6 to 6
- routes: int32 [4096, 2], P(('node', 'expert')), may hold values from 0 to 3, all different within a row; in each aligned block of 128 rows (0 to 127, 128 to 255, ...) at most 96 rows name the same one
- plan: int32 [4], replicated, may hold values from 0 to 5
Outputs:
- gossiped_gu: bfloat16 [32768, 1024], P('node', 'expert')
- gossiped_down: bfloat16 [1024, 16384], P('node', 'expert')
- averaged_gu: float32 [4096, 1024], P('node', 'expert')
- averaged_down: float32 [128, 16384], P('node', 'expert')
Inputs may be any that keep to these rules, and one draw needn't show every extreme that they name: `routes`: each row names 2 different experts; the rows of one device name one expert 96 times at most.
All inputs are finite; a program needn't handle non-finite values.
Results may differ from a plain program's by a relative error of at most 0.0078.
Values may be sent and summed in bfloat16 or wider, within the bound.
A program may use at most 128 MiB of HBM per device.

v0:
```python
import math

import jax
import jax.numpy as jnp
from jax import lax
from jax.sharding import PartitionSpec as P


def everyone(value, axis):
    count = lax.axis_size(axis)
    spread = jnp.broadcast_to(value[None], (count,) + value.shape)
    return lax.all_to_all(spread, axis, 0, 0)


def body(param_gu, param_down, tokens, cotangent, routes, plan):
    nodes = lax.axis_size("node")
    width = tokens.shape[1]
    hid = param_down.shape[0]
    mine = lax.axis_index("expert")
    rows = everyone(tokens, "expert").reshape(-1, width)
    douts = everyone(cotangent, "expert").reshape(-1, width)
    chosen = lax.all_gather(routes, "expert", axis=0, tiled=True)
    picked = jnp.any(chosen == mine, axis=1)[:, None]
    wgu = param_gu.astype(jnp.bfloat16)
    wdown = param_down.astype(jnp.bfloat16)
    both = jnp.dot(rows, wgu, preferred_element_type=jnp.float32) * (1.0 / math.sqrt(width))
    gate = both[:, :hid]
    upper = both[:, hid:]
    sigma = jax.nn.sigmoid(gate)
    act = jnp.where(picked, gate * sigma * upper, 0.0).astype(jnp.bfloat16)
    dact = jnp.dot(douts, wdown.T, preferred_element_type=jnp.float32) * (1.0 / math.sqrt(hid))
    dgate = dact * upper * sigma * (1.0 + gate * (1.0 - sigma))
    dupper = dact * gate * sigma
    dboth = jnp.where(picked, jnp.concatenate([dgate, dupper], axis=1), 0.0).astype(jnp.bfloat16)
    grad_down = jnp.dot(act.T, douts, preferred_element_type=jnp.float32) * (1.0 / math.sqrt(hid))
    grad_gu = jnp.dot(rows.T, dboth, preferred_element_type=jnp.float32) * (1.0 / math.sqrt(width))
    state_gu = (param_gu - 0.5 * grad_gu).astype(jnp.bfloat16)
    state_down = (param_down - 0.5 * grad_down).astype(jnp.bfloat16)

    distance = jnp.left_shift(jnp.int32(1), plan) % nodes
    ranks = jnp.arange(nodes)
    mixing = jnp.eye(nodes, dtype=jnp.float32)
    for step in range(plan.shape[0]):
        mixing = 0.5 * (mixing + jnp.take(mixing, (ranks + distance[step]) % nodes, axis=0))

    def gossip(state):
        split = state.reshape(nodes, -1, state.shape[1])
        held = lax.all_to_all(split, "node", 0, 0)
        mean = jnp.mean(held.astype(jnp.float32), axis=0)
        mixed = jnp.einsum("nm,mrc->nrc", mixing.astype(jnp.bfloat16), held, preferred_element_type=jnp.float32)
        back = lax.all_to_all(mixed.astype(jnp.bfloat16), "node", 0, 0)
        return back.reshape(state.shape), mean

    gossiped_down, averaged_down = gossip(state_down)
    gossiped_gu, averaged_gu = gossip(state_gu)
    return (gossiped_gu, gossiped_down, averaged_gu, averaged_down)


def solution(mesh):
    both = P("node", "expert")
    rows = P(("node", "expert"), None)
    return jax.shard_map(body, mesh=mesh, in_specs=(both, both, rows, rows, rows, P()), out_specs=(both,) * 4, check_vma=False)
```

profile of v0, /device:TPU:9, one launch (start us, length us, event | category | flops | bytes accessed | tf_op | source)
XLA Modules:
  0.0 288.6 jit_solution(8561279933186469785)
XLA Ops:
  0.6 1.7 broadcast_in_dim.48
  2.4 51.3 %all_to_all.30 = bf16[4,128,4096]{2,1,0:T(8,128)(2,1)} all-to-all(bf16[4,128,4096]{2,1,0:T(8,128)(2,1)S(1)} %broadcast_in_dim.48), channel_id=1, replica_groups=mesh['node'=8,'expert'=4] {'expert'}, dimensions={0} | all-to-all | bytes 8388608 | tf_op jit(solution)/shard_map/all_to_all | solution.py:12
  53.7 2.5 broadcast_in_dim.47
  56.2 6.0 %all-to-all-start = ((bf16[4,128,4096]{2,1,0:T(8,128)(2,1)}), bf16[4,128,4096]{2,1,0:T(8,128)(2,1)}, u32[]{:S(2)}, u32[]{:S(2)}) async-start(bf16[4,128,4096]{2,1,0:T(8,128)(2,1)} %broadcast_in_dim.47), calls=%async_computation | async-start | bytes 8388608 | tf_op jit(solution)/shard_map/all_to_all | solution.py:12
  62.1 48.9 %all_gather.3 = s32[512,2]{0,1:T(2,128)S(1)} all-gather(s32[128,2]{0,1:T(2,128)S(1)} %copy-done.4), channel_id=1, replica_groups=mesh['node'=8,'expert'=4] {'expert'}, dimensions={0}, use_global_device_ids=true | all-gather | bytes 5120 | tf_op jit(solution)/shard_map/all_gather | solution.py:22
  111.1 4.9 %fusion.12 = f32[512,256]{0,1:T(8,128)S(1)} fusion(bf16[512,4096]{1,0:T(8,128)(2,1)} %bitcast.24, f32[4096,256]{1,0:T(8,128)} %param.8), kind=kOutput, calls=%fused_computation.19 | convolution fusion | flops 1074921472 | bytes 8912896 | tf_op jit(solution)/shard_map/dot_general | solution.py:26
  116.0 0.0 copy-start.3
  116.0 4.1 %fusion.4 = bf16[128,4096]{1,0:T(8,128)(2,1)} fusion(f32[128,4096]{1,0:T(8,128)S(1)} %copy-done.1, bf16[512,4096]{1,0:T(8,128)(2,1)} %bitcast.5, f32[512,256]{0,1:T(8,128)S(1)} %fusion.12, pred[512]{0:T(512)(128)(4,1)S(1)} %compare_reduce_fusion), kind=kOutput, calls=%fused_computation.10 | convolution fusion | flops 538902528 | bytes 7864832 | tf_op jit(solution)/shard_map/dot_general | solution.py:35
  120.1 5.7 %all-to-all-start.4 = ((bf16[8,16,4096]{2,1,0:T(8,128)(2,1)}), bf16[8,16,4096]{2,1,0:T(8,128)(2,1)S(1)}, u32[]{:S(2)}, u32[]{:S(2)}) async-start(bf16[8,16,4096]{2,1,0:T(8,128)(2,1)} %bitcast.27), calls=%async_computation.4 | async-start | bytes 2097152 | tf_op jit(solution)/shard_map/all_to_all | solution.py:48
  125.8 5.6 %copy.18 = f32[4096,256]{0,1:T(8,128)} copy(f32[4096,256]{1,0:T(8,128)} %param.8) | data formatting | bytes 8388608 | tf_op args[0]
  131.4 4.0 %add_multiply_fusion = (bf16[512,128]{0,1:T(8,128)(2,1)S(1)}, bf16[512,128]{0,1:T(8,128)(2,1)S(1)}) fusion(f32[512,256]{0,1:T(8,128)} %copy-done.3, bf16[512,4096]{1,0:T(8,128)(2,1)} %bitcast.5, f32[128,4096]{1,0:T(8,128)S(1)} %copy-done.1), kind=kOutput, calls=%fused_computation.29 | convolution fusion | flops 538312704 | bytes 7077888 | tf_op jit(solution)/shard_map/dot_general | solution.py:31
  135.5 3.5 %fusion.2 = bf16[4096,256]{0,1:T(8,128)(2,1)S(1)} fusion(f32[4096,256]{0,1:T(8,128)} %copy.18, bf16[512,4096]{1,0:T(8,128)(2,1)S(1)} %bitcast.25, bf16[512,128]{0,1:T(8,128)(2,1)S(1)} %get-tuple-element.6, bf16[512,128]{0,1:T(8,128)(2,1)S(1)} %get-tuple-element.5, pred[512]{0:T(512)(128)(4,1)S(1)} %compare_reduce_fusion), kind=kOutput, calls=%fused_computation.7 | convolution fusion | flops 1077542912 | bytes 10748416 | tf_op jit(solution)/shard_map/dot_general | solution.py:36
  138.9 0.0 copy-start.5
  139.0 2.5 copy.24
  141.4 8.0 %all-to-all-done.4 = bf16[8,16,4096]{2,1,0:T(8,128)(2,1)S(1)} async-done(((bf16[8,16,4096]{2,1,0:T(8,128)(2,1)}), bf16[8,16,4096]{2,1,0:T(8,128)(2,1)S(1)}, u32[]{:S(2)}, u32[]{:S(2)}) %all-to-all-start.4) | async-done | bytes 1048608 | tf_op jit(solution)/shard_map/all_to_all | solution.py:48
  149.4 5.9 %all-to-all-start.2 = ((bf16[8,512,256]{2,1,0:T(8,128)(2,1)}), bf16[8,512,256]{2,1,0:T(8,128)(2,1)S(1)}, u32[]{:S(2)}, u32[]{:S(2)}) async-start(bf16[8,512,256]{2,1,0:T(8,128)(2,1)} %bitcast.26), calls=%async_computation.2 | async-start | bytes 4194304 | tf_op jit(solution)/shard_map/all_to_all | solution.py:48
  155.4 0.6 fusion.40
  156.0 0.6 compare_select_fusion.3
  156.7 0.6 gather_fusion
  157.2 0.6 compare_and_fusion.3
  157.9 0.7 compare_select_fusion.2
  158.5 0.1 fusion.28
  158.6 0.6 gather_fusion.1
  159.2 0.7 compare_and_fusion.2
  159.8 0.7 compare_select_fusion.1
  160.5 0.1 fusion.27
  160.6 0.6 gather_fusion.2
  161.2 0.7 compare_and_fusion.1
  161.8 0.7 compare_select_fusion
  162.5 0.1 fusion.26
  162.6 0.6 gather_fusion.3
  163.1 0.7 compare_and_fusion
  163.8 0.1 fusion.30
  163.9 1.3 convolution_convert_fusion
  165.1 1.6 copy.23
  166.7 35.2 %all-to-all-done.2 = bf16[8,512,256]{2,1,0:T(8,128)(2,1)S(1)} async-done(((bf16[8,512,256]{2,1,0:T(8,128)(2,1)}), bf16[8,512,256]{2,1,0:T(8,128)(2,1)S(1)}, u32[]{:S(2)}, u32[]{:S(2)}) %all-to-all-start.2) | async-done | bytes 2097184 | tf_op jit(solution)/shard_map/all_to_all | solution.py:48
  201.9 5.5 %all-to-all-start.5 = ((bf16[8,16,4096]{2,1,0:T(8,128)(2,1)}), bf16[8,16,4096]{2,1,0:T(8,128)(2,1)}, u32[]{:S(2)}, u32[]{:S(2)}) async-start(bf16[8,16,4096]{2,1,0:T(8,128)(2,1)} %copy.23), calls=%async_computation.5 | async-start | bytes 2097152 | tf_op jit(solution)/shard_map/all_to_all | solution.py:51
  207.4 1.3 fusion.9
  208.8 1.7 copy.21
  210.5 19.6 %all-to-all-done.5 = bf16[8,16,4096]{2,1,0:T(8,128)(2,1)} async-done(((bf16[8,16,4096]{2,1,0:T(8,128)(2,1)}), bf16[8,16,4096]{2,1,0:T(8,128)(2,1)}, u32[]{:S(2)}, u32[]{:S(2)}) %all-to-all-start.5) | async-done | bytes 1048608 | tf_op jit(solution)/shard_map/all_to_all | solution.py:51
  230.1 7.0 %all-to-all-start.3 = ((bf16[8,512,256]{2,1,0:T(8,128)(2,1)}), bf16[8,512,256]{2,1,0:T(8,128)(2,1)}, u32[]{:S(2)}, u32[]{:S(2)}) async-start(bf16[8,512,256]{2,1,0:T(8,128)(2,1)} %copy.21), calls=%async_computation.3 | async-start | bytes 4194304 | tf_op jit(solution)/shard_map/all_to_all | solution.py:51
  237.1 0.1 convert_reduce_fusion.1
  237.2 0.7 broadcast_multiply_fusion.1
  238.0 0.3 convert_reduce_fusion
  238.2 0.8 broadcast_multiply_fusion
  239.1 44.2 %all-to-all-done.3 = bf16[8,512,256]{2,1,0:T(8,128)(2,1)} async-done(((bf16[8,512,256]{2,1,0:T(8,128)(2,1)}), bf16[8,512,256]{2,1,0:T(8,128)(2,1)}, u32[]{:S(2)}, u32[]{:S(2)}) %all-to-all-start.3) | async-done | bytes 2097184 | tf_op jit(solution)/shard_map/all_to_all | solution.py:51
  283.3 3.0 %copy.33 = bf16[4096,256]{1,0:T(8,128)(2,1)} copy(bf16[4096,256]{1,0:T(8,128)(2,1)} %bitcast.9) | data formatting | bytes 4194304
  286.3 2.3 copy.34
  (18 shorter events, 0.1 us)
Async XLA Ops:
  2.4 51.3 %copy-start.2 = (bf16[128,4096]{1,0:T(8,128)(2,1)S(1)}, bf16[128,4096]{1,0:T(8,128)(2,1)}, u32[]{:S(2)}) copy-start(bf16[128,4096]{1,0:T(8,128)(2,1)} %param.11) | copy-start | bytes 3145732
  56.2 6.0 %copy-start.4 = (s32[128,2]{0,1:T(2,128)S(1)}, s32[128,2]{0,1:T(2,128)}, u32[]{:S(2)}) copy-start(s32[128,2]{0,1:T(2,128)} %param.12) | copy-start | bytes 3076
  56.2 59.8 %all-to-all-start = ((bf16[4,128,4096]{2,1,0:T(8,128)(2,1)}), bf16[4,128,4096]{2,1,0:T(8,128)(2,1)}, u32[]{:S(2)}, u32[]{:S(2)}) async-start(bf16[4,128,4096]{2,1,0:T(8,128)(2,1)} %broadcast_in_dim.47), calls=%async_computation | async-start | bytes 8388608 | tf_op jit(solution)/shard_map/all_to_all | solution.py:12
  111.1 4.9 %copy-start.1 = (f32[128,4096]{1,0:T(8,128)S(1)}, f32[128,4096]{1,0:T(8,128)}, u32[]{:S(2)}) copy-start(f32[128,4096]{1,0:T(8,128)} %param.9) | copy-start | bytes 6291460
  116.0 4.1 %copy-start.3 = (f32[512,256]{0,1:T(8,128)}, f32[512,256]{0,1:T(8,128)S(1)}, u32[]{:S(2)}) copy-start(f32[512,256]{0,1:T(8,128)S(1)} %fusion.12) | copy-start | bytes 1572868
  120.1 29.3 %all-to-all-start.4 = ((bf16[8,16,4096]{2,1,0:T(8,128)(2,1)}), bf16[8,16,4096]{2,1,0:T(8,128)(2,1)S(1)}, u32[]{:S(2)}, u32[]{:S(2)}) async-start(bf16[8,16,4096]{2,1,0:T(8,128)(2,1)} %bitcast.27), calls=%async_computation.4 | async-start | bytes 2097152 | tf_op jit(solution)/shard_map/all_to_all | solution.py:48
  131.4 4.0 %copy-start = (bf16[4,128,4096]{2,1,0:T(8,128)(2,1)S(1)}, bf16[4,128,4096]{2,1,0:T(8,128)(2,1)}, u32[]{:S(2)}) copy-start(bf16[4,128,4096]{2,1,0:T(8,128)(2,1)} %all_to_all.30) | copy-start | bytes 12582916
  138.9 16.4 %copy-start.5 = (s32[4]{0:T(128)S(1)}, s32[4]{0:T(128)}, u32[]{:S(2)}) copy-start(s32[4]{0:T(128)} %param.13) | copy-start | bytes 52
  149.4 52.5 %all-to-all-start.2 = ((bf16[8,512,256]{2,1,0:T(8,128)(2,1)}), bf16[8,512,256]{2,1,0:T(8,128)(2,1)S(1)}, u32[]{:S(2)}, u32[]{:S(2)}) async-start(bf16[8,512,256]{2,1,0:T(8,128)(2,1)} %bitcast.26), calls=%async_computation.2 | async-start | bytes 4194304 | tf_op jit(solution)/shard_map/all_to_all | solution.py:48
  201.9 28.2 %all-to-all-start.5 = ((bf16[8,16,4096]{2,1,0:T(8,128)(2,1)}), bf16[8,16,4096]{2,1,0:T(8,128)(2,1)}, u32[]{:S(2)}, u32[]{:S(2)}) async-start(bf16[8,16,4096]{2,1,0:T(8,128)(2,1)} %copy.23), calls=%async_computation.5 | async-start | bytes 2097152 | tf_op jit(solution)/shard_map/all_to_all | solution.py:51
  230.1 53.2 %all-to-all-start.3 = ((bf16[8,512,256]{2,1,0:T(8,128)(2,1)}), bf16[8,512,256]{2,1,0:T(8,128)(2,1)}, u32[]{:S(2)}, u32[]{:S(2)}) async-start(bf16[8,512,256]{2,1,0:T(8,128)(2,1)} %copy.21), calls=%async_computation.3 | async-start | bytes 4194304 | tf_op jit(solution)/shard_map/all_to_all | solution.py:51
where the time goes:
time: 293 us; the launch traced here: 289 us
  waiting for transfers between devices  107 us (37%)
  blocking collectives  100 us (34%)
  starting transfers between devices  30.1 us (10%)
  local copies, waits for them, and re-layouts  23.8 us (8%)
  matrix products  19 us (6%)
  other arithmetic  7.57 us (3%)
    all_to_all x2, waiting for transfers between devices, gossip(): back = lax.all_to_all(mixed.astype(jnp.bfloat16), 'node', 0, 0)  63.8 us
    all_to_all x1, blocking collectives, everyone(): return lax.all_to_all(spread, axis, 0, 0)  51.3 us
    all_gather x1, blocking collectives, body(): chosen = lax.all_gather(routes, 'expert', axis=0, tiled=True)  48.9 us
    all_to_all x2, waiting for transfers between devices, gossip(): held = lax.all_to_all(split, 'node', 0, 0)  43.3 us
    all_to_all x2, starting transfers between devices, gossip(): back = lax.all_to_all(mixed.astype(jnp.bfloat16), 'node', 0, 0)  12.5 us
    all_to_all x2, starting transfers between devices, gossip(): held = lax.all_to_all(split, 'node', 0, 0)  11.6 us
    unnamed x15, local copies, waits for them, and re-layouts  11 us
    all_to_all x1, starting transfers between devices, everyone(): return lax.all_to_all(spread, axis, 0, 0)  5.96 us
  transfers between devices with their start and end apart: 5, of which 4 were waited for; matrix products, arithmetic and copies ran while one was open for 13% of the time, Pallas kernels for 0%

commit v1 on v0

--- a/solution.py
+++ b/solution.py
@@ -1,8 +1,11 @@
+from functools import partial
 import math
 
 import jax
 import jax.numpy as jnp
 from jax import lax
+from jax.experimental import pallas as pl
+from jax.experimental.pallas import tpu as pltpu
 from jax.sharding import PartitionSpec as P
 
 
@@ -12,7 +15,7 @@
     return lax.all_to_all(spread, axis, 0, 0)
 
 
-def body(param_gu, param_down, tokens, cotangent, routes, plan):
+def plain_body(param_gu, param_down, tokens, cotangent, routes, plan):
     nodes = lax.axis_size("node")
     width = tokens.shape[1]
     hid = param_down.shape[0]
@@ -56,6 +59,355 @@
     return (gossiped_gu, gossiped_down, averaged_gu, averaged_down)
 
 
+X_CHUNKS = 2
+DY_CHUNKS = 4
+GU_CHUNKS = 4
+DOWN_CHUNKS = 2
+MESH = pl.DeviceIdType.MESH
+
+
+def mixing_of(plan, nodes):
+    ranks = jnp.arange(nodes)
+    mixing = jnp.eye(nodes, dtype=jnp.float32)
+    distance = jnp.left_shift(jnp.int32(1), plan) % nodes
+    for step in range(plan.shape[0]):
+        shifted = (ranks[:, None] + distance[step]) % nodes == ranks[None, :]
+        mixing = 0.5 * (mixing + jnp.dot(shifted.astype(jnp.float32), mixing, precision="highest"))
+    return mixing
+
+
+def kernel(nodes, mix_ref, gu_in, down_in, x_in, dy_in, pick_in, og_gu, og_down, avg_gu, avg_down,
+           par_gu, par_down, xs, dys, xt, picks, wgu, wdown, both_s, act_s, dgu_s,
+           p_gu, p_down, l_gu, l_down, t_gu, t_down, m_gu, m_down,
+           loc_sem, tok_send, tok_recv, pick_send, pick_recv, a_send, a_recv):
+    me = lax.axis_index("node")
+    e = lax.axis_index("expert")
+    deep = nodes // 2
+    z, x = lax.div(me, 2), lax.rem(me, 2)
+    partner = e + 1 - 2 * lax.rem(e, 2)
+    cross = lax.rem(e + 2, 4)
+    diag = partner + 2 - 4 * lax.div(partner, 2)
+    tok, width = x_in.shape
+    hid = down_in.shape[0]
+
+    def node_at(dz, dx):
+        return lax.rem(z + dz + deep, deep) * 2 + lax.rem(x + dx, 2)
+
+    barrier = pltpu.get_barrier_semaphore()
+    offsets = [(dz, dx) for dz in range(deep) for dx in range(2)][1:]
+    for other in (partner, cross, diag):
+        pl.semaphore_signal(barrier, inc=1, device_id={"expert": other}, device_id_type=MESH)
+    for dz, dx in offsets:
+        pl.semaphore_signal(barrier, inc=1, device_id={"node": node_at(dz, dx)}, device_id_type=MESH)
+
+    local = [
+        pltpu.make_async_copy(x_in, xs.at[0], loc_sem.at[0]),
+        pltpu.make_async_copy(gu_in, par_gu, loc_sem.at[1]),
+        pltpu.make_async_copy(down_in, par_down, loc_sem.at[2]),
+        pltpu.make_async_copy(dy_in, dys.at[0], loc_sem.at[3]),
+    ]
+    for copy in local:
+        copy.start()
+    pl.semaphore_wait(barrier, 3 + len(offsets))
+
+    def piece(which, k):
+        if which == 0:
+            size = tok // X_CHUNKS
+            return (pl.ds(k * size, size), slice(None))
+        size = width // DY_CHUNKS
+        return (slice(None), pl.ds(k * size, size))
+
+    def token_copy(which, k, route):
+        part = piece(which, k)
+        buf = (xs, dys)[which]
+        at = (0 if which == 0 else X_CHUNKS) + k
+        if route == 2:
+            src = buf.at[(2,) + part]
+        else:
+            src = (x_in, dy_in)[which].at[part]
+        return pltpu.make_async_remote_copy(
+            src, buf.at[(route + 1,) + part], tok_send.at[at, route], tok_recv.at[at, route],
+            device_id={"expert": cross if route == 1 else partner}, device_id_type=MESH)
+
+    def pick_copy(i):
+        return pltpu.make_async_remote_copy(
+            pick_in, picks.at[i], pick_send.at[i], pick_recv.at[i],
+            device_id={"expert": (partner, cross, diag)[i]}, device_id_type=MESH)
+
+    order = [(0, k) for k in range(X_CHUNKS)] + [(1, k) for k in range(DY_CHUNKS)]
+    token_copies = {}
+    for which, k in order:
+        if (which, k) == (1, 0):
+            for i in range(3):
+                pick_copy(i).start()
+        for route in (1, 0):
+            token_copy(which, k, route).start()
+
+    def picked(slot):
+        held = pick_in[...] if slot == 0 else picks[slot - 1]
+        lane = lax.broadcasted_iota(jnp.int32, held.shape, 1)
+        return jnp.sum(jnp.where(lane == e, held.astype(jnp.float32), 0.0), axis=1, keepdims=True)
+
+    def forward_x(slot):
+        rows = pl.ds(slot * tok, tok)
+        both_s[rows, :] = jnp.dot(xs[slot], wgu[...], preferred_element_type=jnp.float32) * (1.0 / math.sqrt(width))
+
+    def turn_x(slot):
+        span = 512
+        for at in range(0, width, span):
+            xt[pl.ds(at, span), pl.ds(slot * tok, tok)] = xs[slot, :, at:at + span].T
+
+    def activate(slot):
+        rows = pl.ds(slot * tok, tok)
+        gate, upper = both_s[rows, :hid], both_s[rows, hid:]
+        act = gate * jax.nn.sigmoid(gate) * upper * picked(slot)
+        act_s[:, rows] = act.T.astype(jnp.bfloat16)
+
+    def backward(slot):
+        rows = pl.ds(slot * tok, tok)
+        gate, upper = both_s[rows, :hid], both_s[rows, hid:]
+        sigma = jax.nn.sigmoid(gate)
+        dact = lax.dot_general(dys[slot], wdown[...], (((1,), (1,)), ((), ())), preferred_element_type=jnp.float32)
+        dact = dact * (1.0 / math.sqrt(hid)) * picked(slot)
+        dgu_s[rows, :hid] = (dact * upper * sigma * (1.0 + gate * (1.0 - sigma))).astype(jnp.bfloat16)
+        dgu_s[rows, hid:] = (dact * gate * sigma).astype(jnp.bfloat16)
+
+    gu_rows, down_rows = width // nodes, hid // nodes
+    gu_part, down_part = gu_rows // GU_CHUNKS, width // DOWN_CHUNKS
+    chunks = [("down", j) for j in range(DOWN_CHUNKS)] + [("gu", c) for c in range(GU_CHUNKS)]
+
+    def piece_of(kind, c, ref, owner):
+        if kind == "gu":
+            return ref.at[pl.ds(owner * gu_rows + c * gu_part, gu_part), :]
+        return ref.at[pl.ds(owner * down_rows, down_rows), pl.ds(c * down_part, down_part)]
+
+    def places(phase, kind, c):
+        p, l, m, og = (p_gu, l_gu, m_gu, og_gu) if kind == "gu" else (p_down, l_down, m_down, og_down)
+        if phase == 0:
+            return (lambda to: piece_of(kind, c, p, to)), (lambda of: l.at[c, of])
+        return (lambda to: m.at[c, to]), (lambda of: piece_of(kind, c, og, of))
+
+    relayed = (deep // 2, 1)
+
+    def send(phase, kind, c, i):
+        dz, dx = offsets[i]
+        source, lands = places(phase, kind, c)
+        at = phase * len(chunks) + chunks.index((kind, c))
+        to = node_at(dz, dx)
+        via, dst = to, lands(me)
+        if (dz, dx) == relayed:
+            via = node_at(-1, 0)
+            dst = (t_gu if kind == "gu" else t_down).at[phase, c]
+        return pltpu.make_async_remote_copy(
+            source(to), dst, a_send.at[at, i], a_recv.at[at, i], device_id={"node": via}, device_id_type=MESH)
+
+    def pass_on(phase, kind, c):
+        at = phase * len(chunks) + chunks.index((kind, c))
+        lands = places(phase, kind, c)[1]
+        return pltpu.make_async_remote_copy(
+            (t_gu if kind == "gu" else t_down).at[phase, c], lands(node_at(1, 0)),
+            a_send.at[at, len(offsets)], a_recv.at[at, len(offsets)],
+            device_id={"node": node_at(relayed[0] + 1, relayed[1])}, device_id_type=MESH)
+
+    first = [offsets.index(relayed)] + [i for i, o in enumerate(offsets) if o != relayed]
+
+    def send_all(phase, kind, c):
+        for i in first:
+            send(phase, kind, c, i).start()
+
+    def relay(phase, kind, c):
+        send(phase, kind, c, first[0]).wait_recv()
+        pass_on(phase, kind, c).start()
+
+    def arrived(phase, kind, c):
+        for i in first[1:]:
+            send(phase, kind, c, i).wait_recv()
+        pass_on(phase, kind, c).wait_recv()
+
+    def sent(phase, kind, c):
+        for i in first:
+            send(phase, kind, c, i).wait_send()
+        pass_on(phase, kind, c).wait_send()
+
+    def mix_block(parts):
+        total = parts[0]
+        for part in parts[1:]:
+            total = total + part
+        mixed = []
+        for to in range(nodes):
+            acc = parts[0] * mix_ref[to, 0]
+            for of in range(1, nodes):
+                acc = acc + parts[of] * mix_ref[to, of]
+            mixed.append(acc.astype(jnp.bfloat16))
+        return total * (1.0 / nodes), mixed
+
+    def own(kind, c):
+        if kind == "gu":
+            return pltpu.make_async_copy(m_gu.at[c, me], piece_of(kind, c, og_gu, me), loc_sem.at[4 + c])
+        return pltpu.make_async_copy(m_down.at[c, me], piece_of(kind, c, og_down, me), loc_sem.at[4 + GU_CHUNKS + c])
+
+    def mix(kind, c):
+        if kind == "gu":
+            tall, wide = math.gcd(32, gu_part), 128
+
+            def step(b, carry):
+                rows = pl.ds(pl.multiple_of(b * tall, tall), tall)
+                for at in range(0, 2 * hid, wide):
+                    parts = [l_gu[c, of, rows, at:at + wide].astype(jnp.float32) for of in range(nodes)]
+                    mean, mixed = mix_block(parts)
+                    avg_gu[pl.ds(pl.multiple_of(c * gu_part + b * tall, tall), tall), at:at + wide] = mean
+                    for to in range(nodes):
+                        m_gu[c, to, rows, at:at + wide] = mixed[to]
+                return carry
+            lax.fori_loop(0, gu_part // tall, step, 0)
+        else:
+            wide = 256
+
+            def step(b, carry):
+                cols = pl.ds(pl.multiple_of(b * wide, wide), wide)
+                parts = [l_down[c, of, :, cols].astype(jnp.float32) for of in range(nodes)]
+                mean, mixed = mix_block(parts)
+                avg_down[:, pl.ds(pl.multiple_of(c * down_part + b * wide, wide), wide)] = mean
+                for to in range(nodes):
+                    m_down[c, to, :, cols] = mixed[to]
+                return carry
+            lax.fori_loop(0, down_part // wide, step, 0)
+
+    def finish(kind, c):
+        arrived(0, kind, c)
+        mix(kind, c)
+        send_all(1, kind, c)
+        own(kind, c).start()
+
+    local[1].wait()
+    wgu[...] = par_gu[...].astype(jnp.bfloat16)
+    local[2].wait()
+    wdown[...] = par_down[...].astype(jnp.bfloat16)
+    local[0].wait()
+    forward_x(0)
+    turn_x(0)
+    for k in range(X_CHUNKS):
+        token_copy(0, k, 0).wait_recv()
+    forward_x(1)
+    local[3].wait()
+    for k in range(X_CHUNKS):
+        token_copy(0, k, 1).wait_recv()
+        token_copy(0, k, 2).start()
+        if k == 0:
+            turn_x(1)
+    for i in range(3):
+        pick_copy(i).wait_recv()
+    forward_x(2)
+    for slot in range(3):
+        activate(slot)
+    for k in range(X_CHUNKS):
+        token_copy(0, k, 2).wait_recv()
+    forward_x(3)
+    activate(3)
+    per_down = DY_CHUNKS // DOWN_CHUNKS
+    for k in range(DY_CHUNKS):
+        token_copy(1, k, 0).wait_recv()
+        token_copy(1, k, 1).wait_recv()
+        token_copy(1, k, 2).start()
+        if k == 0:
+            backward(0)
+            turn_x(2)
+        if k == 1:
+            turn_x(3)
+        token_copy(1, k, 2).wait_recv()
+        size = width // DY_CHUNKS
+        cols = slice(k * size, (k + 1) * size)
+        grad = jnp.dot(act_s[:, :tok], dys[0, :, cols], preferred_element_type=jnp.float32)
+        for slot in range(1, 4):
+            grad = grad + jnp.dot(act_s[:, slot * tok:(slot + 1) * tok], dys[slot, :, cols], preferred_element_type=jnp.float32)
+        p_down[:, cols] = (par_down[:, cols] - grad * (0.5 / math.sqrt(hid))).astype(jnp.bfloat16)
+        if k % per_down == per_down - 1:
+            j = k // per_down
+            span = pl.ds(j * down_part, down_part)
+            l_down[j, me] = p_down[pl.ds(pl.multiple_of(me * down_rows, down_rows), down_rows), span]
+            send_all(0, "down", j)
+    for slot in range(1, 4):
+        backward(slot)
+    relay(0, "down", 0)
+
+    for c in range(GU_CHUNKS):
+        def grad_part(m, carry):
+            rows = pl.ds(pl.multiple_of(m * gu_rows + c * gu_part, gu_part), gu_part)
+            grad = jnp.dot(xt[rows, :], dgu_s[...], preferred_element_type=jnp.float32)
+            p_gu[rows, :] = (par_gu[rows, :] - grad * (0.5 / math.sqrt(width))).astype(jnp.bfloat16)
+            return carry
+        lax.fori_loop(0, nodes, grad_part, 0)
+        l_gu[c, me] = p_gu[pl.ds(pl.multiple_of(me * gu_rows + c * gu_part, gu_part), gu_part), :]
+        send_all(0, "gu", c)
+        if c == 0:
+            relay(0, "down", 1)
+            finish("down", 0)
+    relay(0, "gu", 0)
+    finish("down", 1)
+    queue = [("gu", c) for c in range(GU_CHUNKS)]
+    for c in range(GU_CHUNKS):
+        if c + 1 < GU_CHUNKS:
+            relay(0, "gu", c + 1)
+        finish("gu", c)
+        if c < DOWN_CHUNKS:
+            relay(1, "down", c)
+        else:
+            relay(1, "gu", c - DOWN_CHUNKS)
+    for c in range(GU_CHUNKS - DOWN_CHUNKS, GU_CHUNKS):
+        relay(1, "gu", c)
+    for kind, c in chunks:
+        arrived(1, kind, c)
+        own(kind, c).wait()
+    for kind, c in chunks:
+        sent(0, kind, c)
+        sent(1, kind, c)
+    for which, k in order:
+        for route in range(3):
+            token_copy(which, k, route).wait_send()
+    for i in range(3):
+        pick_copy(i).wait_send()
+
+
+def body(param_gu, param_down, tokens, cotangent, routes, plan):
+    nodes = lax.axis_size("node")
+    groups = lax.axis_size("expert")
+    tok, width = tokens.shape
+    hid = param_down.shape[0]
+    rows = hid // nodes
+    if groups != 4 or nodes % 4 or rows % 16 or (width // nodes) % (16 * GU_CHUNKS):
+        return plain_body(param_gu, param_down, tokens, cotangent, routes, plan)
+    mixing = mixing_of(plan, nodes)
+    pick = jnp.any(routes[:, :, None] == jnp.arange(128, dtype=jnp.int32), axis=1).astype(jnp.bfloat16)
+    bf, f32 = jnp.bfloat16, jnp.float32
+    gu_part, down_part = width // nodes // GU_CHUNKS, width // DOWN_CHUNKS
+    n_chunks = GU_CHUNKS + DOWN_CHUNKS
+    anywhere = pl.BlockSpec(memory_space=pl.ANY)
+    vmem = pl.BlockSpec(memory_space=pltpu.VMEM)
+    return pl.pallas_call(
+        partial(kernel, nodes),
+        out_shape=(
+            jax.ShapeDtypeStruct(param_gu.shape, bf), jax.ShapeDtypeStruct(param_down.shape, bf),
+            jax.ShapeDtypeStruct((width // nodes, 2 * hid), f32), jax.ShapeDtypeStruct((rows, width), f32)),
+        in_specs=[pl.BlockSpec(memory_space=pltpu.SMEM), anywhere, anywhere, anywhere, anywhere, vmem],
+        out_specs=(anywhere, anywhere, vmem, vmem),
+        scratch_shapes=[
+            pltpu.VMEM(param_gu.shape, f32), pltpu.VMEM(param_down.shape, f32),
+            pltpu.VMEM((4, tok, width), bf), pltpu.VMEM((4, tok, width), bf), pltpu.VMEM((width, 4 * tok), bf),
+            pltpu.VMEM((3, tok, 128), bf), pltpu.VMEM(param_gu.shape, bf), pltpu.VMEM(param_down.shape, bf),
+            pltpu.VMEM((4 * tok, 2 * hid), f32), pltpu.VMEM((hid, 4 * tok), bf), pltpu.VMEM((4 * tok, 2 * hid), bf),
+            pltpu.VMEM(param_gu.shape, bf), pltpu.VMEM(param_down.shape, bf),
+            pltpu.VMEM((GU_CHUNKS, nodes, gu_part, 2 * hid), bf), pltpu.VMEM((DOWN_CHUNKS, nodes, rows, down_part), bf),
+            pltpu.VMEM((2, GU_CHUNKS, gu_part, 2 * hid), bf), pltpu.VMEM((2, DOWN_CHUNKS, rows, down_part), bf),
+            pltpu.VMEM((GU_CHUNKS, nodes, gu_part, 2 * hid), bf), pltpu.VMEM((DOWN_CHUNKS, nodes, rows, down_part), bf),
+            pltpu.SemaphoreType.DMA((4 + n_chunks,)),
+            pltpu.SemaphoreType.DMA((X_CHUNKS + DY_CHUNKS, 3)), pltpu.SemaphoreType.DMA((X_CHUNKS + DY_CHUNKS, 3)),
+            pltpu.SemaphoreType.DMA((3,)), pltpu.SemaphoreType.DMA((3,)),
+            pltpu.SemaphoreType.DMA((2 * n_chunks, nodes)), pltpu.SemaphoreType.DMA((2 * n_chunks, nodes)),
+        ],
+        compiler_params=pltpu.CompilerParams(collective_id=1, has_side_effects=True, vmem_limit_bytes=60 * 2**20),
+    )(mixing, param_gu, param_down, tokens, cotangent, pick)
+
+
 def solution(mesh):
     both = P("node", "expert")
     rows = P(("node", "expert"), None)

time: 293 us -> 197 us (0.67); the launches traced: 289 us -> 197 us
  Pallas kernels: 0 us -> 184 us
  waiting for transfers between devices: 107 us -> 0 us
  blocking collectives: 100 us -> 0 us
  starting transfers between devices: 30.1 us -> 0 us
  matrix products: 19 us -> 1.37 us
  local copies, waits for them, and re-layouts: 23.8 us -> 6.6 us
    pallas_call x0 -> x1, Pallas kernels: none -> 184 us  [body(): pl.pallas_call(partial(kernel, nodes), out_shape=(jax.ShapeDtypeStruct(pa...]
    all_to_all x5 -> x0, waiting for transfers between devices: 107 us -> none  [the longest x2 63.8 us: gossip(): back = lax.all_to_all(mixed.astype(jnp.bfloat16), 'node', 0, 0)]
    all_to_all x1 -> x0, blocking collectives: 51.3 us -> none  [everyone(): return lax.all_to_all(spread, axis, 0, 0)]
    all_gather x1 -> x0, blocking collectives: 48.9 us -> none  [body(): chosen = lax.all_gather(routes, 'expert', axis=0, tiled=True)]
    all_to_all x5 -> x0, starting transfers between devices: 30.1 us -> none  [the longest x2 12.5 us: gossip(): back = lax.all_to_all(mixed.astype(jnp.bfloat16), 'node', 0, 0)]
    dot_general x6 -> x4, matrix products: 19 us -> 1.37 us  [mixing_of(): jnp.dot(shifted.astype(jnp.float32), mixing, precision='highest')]
    unnamed x15 -> x10, local copies, waits for them, and re-layouts: 11 us -> 6.01 us
    broadcast_in_dim x2 -> x0, local copies, waits for them, and re-layouts: 4.2 us -> none  [everyone(): spread = jnp.broadcast_to(value[None], (count,) + value.shape)]
  transfers between devices with their start and end apart: 5 -> 0, of which waited for: 4 -> 0; matrix products, arithmetic and copies ran while one was open for 13% -> 0% of each run, Pallas kernels for 0% -> 0%
where the time goes in v1:
time: 197 us
  Pallas kernels  184 us (93%)
  local copies, waits for them, and re-layouts  6.6 us (3%)
  other arithmetic  4.7 us (2%)
    pallas_call x1, Pallas kernels, body(): pl.pallas_call(partial(kernel, nodes), out_shape=(jax.ShapeDtypeStruct(pa...  184 us
    unnamed x10, local copies, waits for them, and re-layouts  6.01 us

profile of v1, /device:TPU:9, one launch (start us, length us, event | category | flops | bytes accessed | tf_op | source)
XLA Modules:
  0.0 197.2 jit_solution(2816768820288064388)
XLA Ops:
  0.6 0.7 and_select_fusion.4
  1.3 0.6 fusion.14
  1.9 0.7 and_select_fusion
  2.5 0.7 and_select_fusion.1
  3.2 0.7 and_select_fusion.2
  3.9 0.7 and_select_fusion.3
  4.5 0.2 fusion.3
  4.7 0.2 fusion
  4.9 0.2 fusion.1
  5.1 0.8 fusion.2.mix_ref
  5.9 0.8 fusion.4
  6.7 0.6 convert_element_type.5.pick_in
  7.3 183.9 %shard_map.93 = (bf16[4096,256]{1,0:T(8,128)(2,1)}, bf16[128,4096]{1,0:T(8,128)(2,1)}, f32[512,256]{1,0:T(8,128)}, f32[16,4096]{1,0:T(8,128)}) custom-call(f32[8,8]{1,0:T(8,128)} %fusion.2.mix_ref, f32[4096,256]{1,0:T(8,128)} %gu_in.1, f32[128,4096]{1,0:T(8,128)} %down_in.1, bf16[128,4096]{1,0:T(8,128)(2,1)} %x_in.1, bf16[128,4096]{1,0:T(8,128)(2,1)} %dy_in.1, ...), custom_call_target="tpu_custom_call" | custom-call | tf_op jit(solution)/shard_map/pallas_call | solution.py:386
  191.2 0.0 copy-start
  191.2 3.1 %copy.15 = bf16[4096,256]{1,0:T(8,128)(2,1)} copy(bf16[4096,256]{1,0:T(8,128)(2,1)} %get-tuple-element.12) | data formatting | bytes 4194304
  194.3 0.0 copy-done
  194.3 0.0 copy-start.1
  194.3 0.0 copy-start.2
  194.3 1.0 copy.16
  195.3 0.4 copy-done.1
  195.7 0.8 copy.17
  196.5 0.0 copy-done.2
  196.5 0.7 copy.18
Async XLA Ops:
  191.2 3.1 %copy-start = (bf16[128,4096]{1,0:T(8,128)(2,1)S(1)}, bf16[128,4096]{1,0:T(8,128)(2,1)}, u32[]{:S(2)}) copy-start(bf16[128,4096]{1,0:T(8,128)(2,1)} %get-tuple-element.13) | copy-start | bytes 3145732
  194.3 1.4 copy-start.1
  194.3 2.2 %copy-start.2 = (f32[16,4096]{1,0:T(8,128)S(1)}, f32[16,4096]{1,0:T(8,128)}, u32[]{:S(2)}) copy-start(f32[16,4096]{1,0:T(8,128)} %get-tuple-element.15) | copy-start | bytes 786436

commit v2 on v1

--- a/solution.py
+++ b/solution.py
@@ -67,13 +67,13 @@
 
 
 def mixing_of(plan, nodes):
+    rounds = plan.shape[0]
     ranks = jnp.arange(nodes)
-    mixing = jnp.eye(nodes, dtype=jnp.float32)
     distance = jnp.left_shift(jnp.int32(1), plan) % nodes
-    for step in range(plan.shape[0]):
-        shifted = (ranks[:, None] + distance[step]) % nodes == ranks[None, :]
-        mixing = 0.5 * (mixing + jnp.dot(shifted.astype(jnp.float32), mixing, precision="highest"))
-    return mixing
+    taken = (jnp.arange(2**rounds)[:, None] >> jnp.arange(rounds)[None, :]) & 1
+    reach = jnp.sum(taken * distance[None, :], axis=1)
+    hits = (ranks[:, None, None] + reach) % nodes == ranks[None, :, None]
+    return jnp.mean(hits.astype(jnp.float32), axis=2)
 
 
 def kernel(nodes, mix_ref, gu_in, down_in, x_in, dy_in, pick_in, og_gu, og_down, avg_gu, avg_down,
@@ -342,19 +342,16 @@
         if c == 0:
             relay(0, "down", 1)
             finish("down", 0)
-    relay(0, "gu", 0)
     finish("down", 1)
-    queue = [("gu", c) for c in range(GU_CHUNKS)]
     for c in range(GU_CHUNKS):
-        if c + 1 < GU_CHUNKS:
-            relay(0, "gu", c + 1)
+        relay(0, "gu", c)
+    for j in range(DOWN_CHUNKS):
+        relay(1, "down", j)
+    for c in range(GU_CHUNKS):
         finish("gu", c)
-        if c < DOWN_CHUNKS:
-            relay(1, "down", c)
-        else:
-            relay(1, "gu", c - DOWN_CHUNKS)
-    for c in range(GU_CHUNKS - DOWN_CHUNKS, GU_CHUNKS):
-        relay(1, "gu", c)
+        if c:
+            relay(1, "gu", c - 1)
+    relay(1, "gu", GU_CHUNKS - 1)
     for kind, c in chunks:
         arrived(1, kind, c)
         own(kind, c).wait()

time: 197 us -> 194 us (0.985)
    select_n x4 -> x1, other arithmetic: 2.63 us -> 0.01 us  [mixing_of(): hits = (ranks[:, None, None] + reach) % nodes == ranks[None, :, None]]
where the time goes in v2:
time: 194 us; the launch traced here: 193 us
  Pallas kernels  184 us (95%)
  local copies, waits for them, and re-layouts  6.01 us (3%)
  other arithmetic  2.86 us (1%)
    pallas_call x1, Pallas kernels, body(): pl.pallas_call(partial(kernel, nodes), out_shape=(jax.ShapeDtypeStruct(pa...  184 us
    unnamed x10, local copies, waits for them, and re-layouts  6.01 us

profile of v2, /device:TPU:9, one launch (start us, length us, event | category | flops | bytes accessed | tf_op | source)
XLA Modules:
  0.0 193.3 jit_solution(12261010059232512046)
XLA Ops:
  0.6 0.7 and_select_fusion
  1.3 0.1 multiply_reduce_fusion
  1.4 0.1 convert_reduce_fusion
  1.5 0.6 broadcast_multiply_fusion.mix_ref
  2.1 0.8 fusion
  2.9 0.6 convert_element_type.7.pick_in
  3.5 183.8 %shard_map.93 = (bf16[4096,256]{1,0:T(8,128)(2,1)}, bf16[128,4096]{1,0:T(8,128)(2,1)}, f32[512,256]{1,0:T(8,128)}, f32[16,4096]{1,0:T(8,128)}) custom-call(f32[8,8]{1,0:T(8,128)} %broadcast_multiply_fusion.mix_ref, f32[4096,256]{1,0:T(8,128)} %gu_in.1, f32[128,4096]{1,0:T(8,128)} %down_in.1, bf16[128,4096]{1,0:T(8,128)(2,1)} %x_in.1, ...), custom_call_target="tpu_custom_call" | custom-call | tf_op jit(solution)/shard_map/pallas_call | solution.py:383
  187.3 0.0 copy-start
  187.3 3.1 %copy.15 = bf16[4096,256]{1,0:T(8,128)(2,1)} copy(bf16[4096,256]{1,0:T(8,128)(2,1)} %get-tuple-element.8) | data formatting | bytes 4194304
  190.5 0.0 copy-done
  190.5 0.0 copy-start.1
  190.5 0.0 copy-start.2
  190.5 1.0 copy.16
  191.4 0.4 copy-done.1
  191.8 0.8 copy.17
  192.6 0.0 copy-done.2
  192.6 0.7 copy.18
  (1 shorter events, 0.0 us)
Async XLA Ops:
  187.3 3.1 %copy-start = (bf16[128,4096]{1,0:T(8,128)(2,1)S(1)}, bf16[128,4096]{1,0:T(8,128)(2,1)}, u32[]{:S(2)}) copy-start(bf16[128,4096]{1,0:T(8,128)(2,1)} %get-tuple-element.9) | copy-start | bytes 3145732
  190.5 1.4 copy-start.1
  190.5 2.2 %copy-start.2 = (f32[16,4096]{1,0:T(8,128)S(1)}, f32[16,4096]{1,0:T(8,128)}, u32[]{:S(2)}) copy-start(f32[16,4096]{1,0:T(8,128)} %get-tuple-element.11) | copy-start | bytes 786436
